TPU v7x, 32 devices: a whole 2x2x4 slice. The times are simulated.
32 devices in a mesh: dp: 4 (over y, core), tensor: 2 (over x), pipe: 4 (over z).
Axes of the slice: x: 2, y: 2, z: 4, core: 2. Of those that a mesh axis runs over, the one named last changes fastest.
Arguments:
- grad_parts: float32 [4, 4, 2, 64, 8192], P('dp', 'pipe', 'tensor'), may hold values from -24 to 24
- drop_flags: int32 [4, 4, 2, 64], P('dp', 'pipe', 'tensor'), may hold values from 0 to 1, as said below
- owner_order: int32 [4], replicated, may hold values from 0 to 3, each once
- step_count: int32 [], replicated, may hold values from 1 to 11
- master: float32 [4, 2, 64, 8192], P('pipe', 'tensor', None, 'dp'), may hold values from -6 to 6
- moment_m: float32 [4, 2, 64, 8192], P('pipe', 'tensor', None, 'dp'), may hold values from -0.15625 to 0.15625
- moment_v: float32 [4, 2, 64, 8192], P('pipe', 'tensor', None, 'dp'), may hold values from 0.0001 to 0.001
Outputs:
- new_master: float32 [4, 2, 64, 8192], P('pipe', 'tensor', None, 'dp')
- new_m: float32 [4, 2, 64, 8192], P('pipe', 'tensor', None, 'dp')
- new_v: float32 [4, 2, 64, 8192], P('pipe', 'tensor', None, 'dp')
- direction: float32 [4, 2, 64, 8192], P('pipe', 'tensor', None, 'dp')
- dropped_total: int32 [], replicated
Inputs may be any that keep to these rules, and one draw needn't show every extreme that they name: `drop_flags`: A row may be flagged by every replica.
All inputs are finite; a program needn't handle non-finite values.
Results may differ from a plain program's by a relative error of at most 0.0003.
Values sent between devices are 32-bit elements; how exact they have to be, the bound alone decides.
No kernel may reach another device: no remote copies, remote signals or barrier semaphores. Data moves between devices by JAX's collectives and lax.ppermute only.
A program may use at most 64 MiB of HBM per device.

v0:
```python
import jax
import jax.numpy as jnp
from jax import lax
from jax.sharding import PartitionSpec as P


def body(grad_parts, drop_flags, owner_order, step_count, master, moment_m, moment_v):
    replicas = lax.axis_size("dp")
    flags = drop_flags[0, 0, 0]
    kept = (1 - flags).astype(jnp.float32)
    local_grad = grad_parts[0, 0, 0]
    rows_here = local_grad.shape[0]
    width = local_grad.shape[1]
    block_cols = width // replicas
    term = local_grad * kept[:, None]
    blocks = jnp.take(term.reshape(rows_here, replicas, block_cols), owner_order, axis=1)
    received = lax.all_to_all(blocks, "dp", split_axis=1, concat_axis=1, tiled=True)
    summed = jnp.sum(received, axis=1)
    count = lax.psum(kept, "dp")
    grad = summed / jnp.maximum(count, 1.0)[:, None]
    square_sum, dropped = lax.psum(
        (jnp.sum(grad * grad), jnp.sum(flags).astype(jnp.float32)), ("dp", "tensor", "pipe")
    )
    entries = rows_here * width * lax.axis_size("tensor") * lax.axis_size("pipe")
    rms = jnp.sqrt(square_sum / entries)
    clip = jnp.minimum(1.0, 0.05 / (rms + 1e-06))
    scaled = clip * grad
    old_m = moment_m[0, 0]
    old_v = moment_v[0, 0]
    weights = master[0, 0]
    new_m = 0.9 * old_m + 0.1 * scaled
    new_v = 0.999 * old_v + 0.001 * scaled * scaled
    steps = step_count.astype(jnp.float32)
    m_hat = new_m / (1.0 - jnp.power(0.9, steps))
    v_hat = new_v / (1.0 - jnp.power(0.999, steps))
    direction = m_hat / (jnp.sqrt(v_hat) + 1e-08) + 0.1 * weights
    new_master = weights - 0.001 * direction
    return (
        new_master[None, None],
        new_m[None, None],
        new_v[None, None],
        direction[None, None],
        dropped.astype(jnp.int32),
    )


def solution(mesh):
    return jax.shard_map(
        body,
        mesh=mesh,
        in_specs=(
            P("dp", "pipe", "tensor", None, None),
            P("dp", "pipe", "tensor", None),
            P(),
            P(),
            P("pipe", "tensor", None, "dp"),
            P("pipe", "tensor", None, "dp"),
            P("pipe", "tensor", None, "dp"),
        ),
        out_specs=(
            P("pipe", "tensor", None, "dp"),
            P("pipe", "tensor", None, "dp"),
            P("pipe", "tensor", None, "dp"),
            P("pipe", "tensor", None, "dp"),
            P(),
        ),
        check_vma=False,
    )
```

profile of v0, /device:TPU:0, one launch (start us, length us, event | category | flops | bytes accessed | tf_op | source)
XLA Modules:
  0.0 91.8 jit_solution(3209272403787313384)
XLA Ops:
  0.6 0.7 compare_select_fusion
  1.3 0.7 compare_and_fusion
  2.0 1.3 %fusion.3 = (s32[]{:T(128)}, f32[64]{0:T(128)S(1)}) fusion(s32[1,1,1,64]{3,2,1,0:T(1,128)} %param.8), kind=kLoop, calls=%fused_computation.16 | loop fusion | flops 191 | bytes 516 | tf_op jit(solution)/shard_map/reduce_sum | solution.py:22
  3.2 2.7 %squeeze.2 = f32[64,4,2048]{2,1,0:T(4,128)S(1)} reshape(f32[1,1,1,64,8192]{4,3,2,1,0:T(8,128)} %param.7) | data formatting | bytes 4194304 | tf_op jit(solution)/shard_map/squeeze | solution.py:11
  5.9 2.6 %copy_multiply_fusion = f32[64,4,2048]{2,0,1:T(8,128)} fusion(f32[64,4,2048]{2,1,0:T(4,128)S(1)} %squeeze.2, f32[64]{0:T(128)S(1)} %get-tuple-element.12), kind=kLoop, calls=%fused_computation.1 | loop fusion | flops 524288 | bytes 4194560 | tf_op jit(solution)/shard_map/mul | solution.py:15
  8.5 2.3 %gather_fusion = f32[4,64,2048]{2,1,0:T(8,128)S(1)} fusion(f32[64,4,2048]{2,0,1:T(8,128)} %copy_multiply_fusion, s32[1024]{0:T(1024)S(1)} %pad_clamp_fusion), kind=kCustom, calls=%fused_computation | custom fusion | bytes 4194320 | tf_op jit(solution)/shard_map/jit(_take)/gather | solution.py:16
  10.8 1.6 %select_bitcast_fusion = f32[64,4,2048]{2,0,1:T(8,128)} fusion(f32[4,64,2048]{2,1,0:T(8,128)S(1)} %gather_fusion, pred[4]{0:T(512)(128)(4,1)S(1)} %compare_and_fusion), kind=kLoop, calls=%fused_computation.2 | loop fusion | flops 524288 | bytes 4194308 | tf_op jit(solution)/shard_map/jit(_take)/select_n | solution.py:16
  12.4 4.3 %all-to-all-start = ((f32[64,4,2048]{2,0,1:T(8,128)}), f32[64,4,2048]{2,0,1:T(8,128)S(1)}, u32[]{:S(2)}, u32[]{:S(2)}) async-start(f32[64,4,2048]{2,0,1:T(8,128)} %select_bitcast_fusion), calls=%async_computation | async-start | bytes 4194304 | tf_op jit(solution)/shard_map/all_to_all | solution.py:17
  16.7 0.0 copy-start
  18.1 25.7 %psum.21 = f32[64]{0:T(128)S(1)} all-reduce(f32[64]{0:T(128)S(1)} %get-tuple-element.12), channel_id=1, replica_groups=mesh['dp'=4,'tensor'=2,'pipe'=4] {'dp'}, use_global_device_ids=true, to_apply=%region_1.2 | all-reduce | flops 64 | bytes 512 | tf_op jit(solution)/shard_map/psum | solution.py:19
  43.8 0.0 all-to-all-done
  43.8 0.2 reduce_sum.29
  44.0 0.8 multiply_reduce_fusion
  44.8 41.6 %all-reduce = (f32[]{:T(128)}, f32[]{:T(128)}) all-reduce(f32[]{:T(128)} %multiply_reduce_fusion, f32[]{:T(128)S(6)} %convert_element_type.22), channel_id=1, replica_groups=mesh['dp'=4,'tensor'=2,'pipe'=4] {'dp','tensor','pipe'}, use_global_device_ids=true, to_apply=%region_3.4 | all-reduce | flops 2 | bytes 16 | tf_op jit(solution)/shard_map/psum | solution.py:21
  87.8 0.0 copy-done
  87.8 2.9 %multiply_subtract_fusion = (f32[1,1,64,2048]{3,2,1,0:T(8,128)}, f32[1,1,64,2048]{3,2,1,0:T(8,128)}, f32[1,1,64,2048]{3,2,1,0:T(8,128)}, f32[1,1,64,2048]{3,2,1,0:T(8,128)}) fusion(f32[1,1,64,2048]{3,2,1,0:T(8,128)S(1)} %copy-done, f32[]{:T(128)S(6)} %sub.24, f32[]{:T(128)S(6)} %sub.23, f32[64]{0:T(128)S(1)} %broadcast_maximum_fusion, ...), kind=kLoop, calls=%fused_computation.7 | loop fusion | flops 2228224 | bytes 4194572 | tf_op jit(solution)/shard_map/sub | solution.py:37
  (2 shorter events, 0.0 us)
Async XLA Ops:
  12.4 31.4 %all-to-all-start = ((f32[64,4,2048]{2,0,1:T(8,128)}), f32[64,4,2048]{2,0,1:T(8,128)S(1)}, u32[]{:S(2)}, u32[]{:S(2)}) async-start(f32[64,4,2048]{2,0,1:T(8,128)} %select_bitcast_fusion), calls=%async_computation | async-start | bytes 4194304 | tf_op jit(solution)/shard_map/all_to_all | solution.py:17
  16.7 71.1 %copy-start = (f32[1,1,64,2048]{3,2,1,0:T(8,128)S(1)}, f32[1,1,64,2048]{3,2,1,0:T(8,128)}, u32[]{:S(2)}) copy-start(f32[1,1,64,2048]{3,2,1,0:T(8,128)} %param.11) | copy-start | bytes 1572868
where the time goes:
time: 92.3 us; the launch traced here: 91.8 us
  blocking collectives  67.3 us (73%)
  other arithmetic  10.7 us (12%)
  local copies, waits for them, and re-layouts  4.94 us (5%)
  between operations  4.63 us (5%)
  starting transfers between devices  4.26 us (5%)
    psum x1, blocking collectives, body(): lax.psum((jnp.sum(grad * grad), jnp.sum(flags).astype(jnp.float32)), ('dp...  41.6 us
    psum x1, blocking collectives, body(): count = lax.psum(kept, 'dp')  25.7 us
    all_to_all x1, starting transfers between devices, body(): lax.all_to_all(blocks, 'dp', split_axis=1, concat_axis=1, tiled=True)  4.26 us
    sub x1, other arithmetic, body(): new_master = weights - 0.001 * direction  2.86 us
    squeeze x1, local copies, waits for them, and re-layouts, body(): local_grad = grad_parts[0, 0, 0]  2.67 us
    mul x1, other arithmetic, body(): term = local_grad * kept[:, None]  2.57 us
    select_n x2, other arithmetic, body(): jnp.take(term.reshape(rows_here, replicas, block_cols), owner_order, axis=1)  2.3 us
    gather x1, local copies, waits for them, and re-layouts, body(): jnp.take(term.reshape(rows_here, replicas, block_cols), owner_order, axis=1)  2.27 us
  transfers between devices with their start and end apart: 1, of which 0 were waited for; matrix products, arithmetic and copies ran while one was open for 0% of the time, Pallas kernels for 0%

commit v1 on v0

--- a/solution.py
+++ b/solution.py
@@ -3,24 +3,54 @@
 from jax import lax
 from jax.sharding import PartitionSpec as P
 
+ALL = ("dp", "tensor", "pipe")
+
 
 def body(grad_parts, drop_flags, owner_order, step_count, master, moment_m, moment_v):
     replicas = lax.axis_size("dp")
+    chips = replicas // 2
+    me = lax.axis_index("dp")
+    chip = me // 2
+    core = me % 2
     flags = drop_flags[0, 0, 0]
     kept = (1 - flags).astype(jnp.float32)
     local_grad = grad_parts[0, 0, 0]
     rows_here = local_grad.shape[0]
     width = local_grad.shape[1]
     block_cols = width // replicas
-    term = local_grad * kept[:, None]
-    blocks = jnp.take(term.reshape(rows_here, replicas, block_cols), owner_order, axis=1)
-    received = lax.all_to_all(blocks, "dp", split_axis=1, concat_axis=1, tiled=True)
-    summed = jnp.sum(received, axis=1)
-    count = lax.psum(kept, "dp")
+
+    mate_pairs = [(j, j ^ 1) for j in range(replicas)]
+
+    def along(step):
+        return [(j, (j // 2 + step) % chips * 2 + j % 2) for j in range(replicas)]
+
+    def block_for(device):
+        start = owner_order[device] * block_cols
+        return lax.dynamic_slice_in_dim(local_grad, start, block_cols, 1) * kept[:, None]
+
+    order = [(chip + step) % chips * 2 for step in range(chips)]
+    for_mate = jnp.stack([block_for(base + 1 - core) for base in order])
+    own = jnp.stack([block_for(base + core) for base in order])
+    pair_sum = own + lax.ppermute(for_mate, "dp", mate_pairs)
+    summed = pair_sum[0]
+    for step in range(1, chips):
+        summed = summed + lax.ppermute(pair_sum[step], "dp", along(step))
+
+    count = kept
+    for step in range(1, chips):
+        count = count + lax.ppermute(kept, "dp", along(step))
+    count = count + lax.ppermute(count, "dp", mate_pairs)
+
     grad = summed / jnp.maximum(count, 1.0)[:, None]
-    square_sum, dropped = lax.psum(
-        (jnp.sum(grad * grad), jnp.sum(flags).astype(jnp.float32)), ("dp", "tensor", "pipe")
-    )
+    lane = lax.broadcasted_iota(jnp.int32, (1, 128), 1)
+    square_here = jnp.sum(grad * grad)
+    dropped_here = jnp.sum(flags).astype(jnp.float32)
+    row = jnp.where(lane == 0, square_here, jnp.where(lane == 1, dropped_here, 0.0))
+    devices = lax.axis_size(ALL)
+    rows = lax.all_to_all(jnp.broadcast_to(row[None], (devices, 1, 128)), ALL, 0, 0, tiled=True)
+    totals = jnp.sum(rows, axis=0)[0]
+    square_sum, dropped = totals[0], totals[1]
+
     entries = rows_here * width * lax.axis_size("tensor") * lax.axis_size("pipe")
     rms = jnp.sqrt(square_sum / entries)
     clip = jnp.minimum(1.0, 0.05 / (rms + 1e-06))

time: 92.3 us -> 49 us (0.53)
  blocking collectives: 67.3 us -> 0 us
  waiting for transfers between devices: 0.01 us -> 21.4 us
  starting transfers between devices: 4.26 us -> 9.65 us
  other arithmetic: 10.7 us -> 7.6 us
  between operations: 4.63 us -> 7.31 us
  local copies, waits for them, and re-layouts: 4.94 us -> 2.67 us
    psum x2 -> x0, blocking collectives: 67.3 us -> none  [the longest x1 41.6 us: body(): lax.psum((jnp.sum(grad * grad), jnp.sum(flags).astype(jnp.float32)), ('dp...]
    ppermute x0 -> x4, waiting for transfers between devices: none -> 15.1 us  [the longest x1 12.3 us: body(): count = count + lax.ppermute(kept, 'dp', along(step))]
    all_to_all x1, waiting for transfers between devices: 0.01 us -> 6.34 us  [body(): lax.all_to_all(jnp.broadcast_to(row[None], (devices, 1, 128)), ALL, 0, 0,...]
    ppermute x0 -> x4, starting transfers between devices: none -> 3.58 us  [the longest x1 2.94 us: body(): summed = summed + lax.ppermute(pair_sum[step], 'dp', along(step))]
    sub x1 -> x0, other arithmetic: 2.86 us -> none  [body(): new_master = weights - 0.001 * direction]
    squeeze x1, local copies, waits for them, and re-layouts: 2.67 us -> 0.04 us  [body(): summed = summed + lax.ppermute(pair_sum[step], 'dp', along(step))]
    gather x1 -> x0, local copies, waits for them, and re-layouts: 2.27 us -> none  [body(): jnp.take(term.reshape(rows_here, replicas, block_cols), owner_order, axis=1)]
    all_to_all x1, starting transfers between devices: 4.26 us -> 6.07 us  [body(): lax.all_to_all(jnp.broadcast_to(row[None], (devices, 1, 128)), ALL, 0, 0,...]
  transfers between devices with their start and end apart: 1 -> 5, of which waited for: 0 -> 4; matrix products, arithmetic and copies ran while one was open for 0% -> 0% of each run, Pallas kernels for 0% -> 0%
where the time goes in v1:
time: 49 us; the launch traced here: 48.6 us
  waiting for transfers between devices  21.4 us (44%)
  starting transfers between devices  9.65 us (20%)
  other arithmetic  7.6 us (16%)
  between operations  7.31 us (15%)
  local copies, waits for them, and re-layouts  2.67 us (5%)
    ppermute x1, waiting for transfers between devices, body(): count = count + lax.ppermute(kept, 'dp', along(step))  12.3 us
    all_to_all x1, waiting for transfers between devices, body(): lax.all_to_all(jnp.broadcast_to(row[None], (devices, 1, 128)), ALL, 0, 0,...  6.34 us
    all_to_all x1, starting transfers between devices, body(): lax.all_to_all(jnp.broadcast_to(row[None], (devices, 1, 128)), ALL, 0, 0,...  6.07 us
    ppermute x1, starting transfers between devices, body(): summed = summed + lax.ppermute(pair_sum[step], 'dp', along(step))  2.94 us
    ppermute x1, waiting for transfers between devices, body(): pair_sum = own + lax.ppermute(for_mate, 'dp', mate_pairs)  2.29 us
    reduce_sum x1, other arithmetic, body(): square_here = jnp.sum(grad * grad)  1.88 us
    mul x1, other arithmetic, block_for(): lax.dynamic_slice_in_dim(local_grad, start, block_cols, 1) * kept[:, None]  1.8 us
    broadcast_in_dim x1, other arithmetic, body(): new_master[None, None]  1.72 us
  transfers between devices with their start and end apart: 5, of which 4 were waited for; matrix products, arithmetic and copies ran while one was open for 0% of the time, Pallas kernels for 0%

profile of v1, /device:TPU:0, one launch (start us, length us, event | category | flops | bytes accessed | tf_op | source)
XLA Modules:
  0.0 48.6 jit_solution(15240563165625163404)
XLA Ops:
  0.7 1.4 %fusion.12 = (s32[1]{0:T(128)}, s32[1]{0:T(128)}, s32[1]{0:T(128)}, s32[1]{0:T(128)}) fusion(s32[4]{0:T(128)} %param.9, s32[]{:T(128)S(6)} %select_n.66, s32[]{:T(128)S(6)} %select_n.69, s32[]{:T(128)S(6)} %select_n.73, s32[]{:T(128)S(6)} %select_n.71), kind=kLoop, calls=%fused_computation.27 | loop fusion | bytes 48 | tf_op jit(solution)/shard_map/dynamic_slice | solution.py:28
  4.7 1.3 %fusion.11 = (s32[]{:T(128)}, f32[64]{0:T(128)S(1)}) fusion(s32[1,1,1,64]{3,2,1,0:T(1,128)} %param.8), kind=kLoop, calls=%fused_computation.26 | loop fusion | flops 191 | bytes 516 | tf_op jit(solution)/shard_map/reduce_sum | solution.py:47
  6.0 1.8 %bitcast_multiply_fusion.3 = (f32[1,64,2048]{2,1,0:T(8,128)S(1)}, f32[1,64,2048]{2,1,0:T(8,128)S(1)}, f32[1,64,2048]{2,1,0:T(8,128)S(1)}, f32[1,64,2048]{2,1,0:T(8,128)S(1)}) fusion(f32[1,1,1,64,8192]{4,3,2,1,0:T(8,128)} %param.7, s32[]{:T(128)S(6)} %select_n.67, f32[64]{0:T(128)S(1)} %get-tuple-element.18, s32[]{:T(128)S(6)} %select_n.70, s32[]{:T(128)S(6)} %select_n.74, ...), kind=kLoop, calls=%fused_computation.11 | loop fusion | flops 524288 | bytes 4194576 | tf_op jit(solution)/shard_map/mul | solution.py:29
  7.8 0.1 pad_maximum_fusion
  7.9 0.6 %collective-permute-start = (f32[2,64,2048]{2,1,0:T(8,128)S(1)}, f32[2,64,2048]{2,1,0:T(8,128)S(1)}, u32[]{:S(2)}, u32[]{:S(2)}) collective-permute-start(f32[2,64,2048]{2,1,0:T(8,128)S(1)} %pad_maximum_fusion), channel_id=1, source_target_pairs={{0,8},{8,0},{16,24},{24,16},{1,9},{9,1},{17,25},{25,17},{2,10},{10... | collective-permute-start | bytes 3145736 | tf_op jit(solution)/shard_map/ppermute | solution.py:34
  8.5 2.3 %collective-permute-done = f32[2,64,2048]{2,1,0:T(8,128)S(1)} collective-permute-done((f32[2,64,2048]{2,1,0:T(8,128)S(1)}, f32[2,64,2048]{2,1,0:T(8,128)S(1)}, u32[]{:S(2)}, u32[]{:S(2)}) %collective-permute-start) | collective-permute-done | bytes 1048608 | tf_op jit(solution)/shard_map/ppermute | solution.py:34
  10.8 0.0 copy-start.3
  10.8 0.2 maximum_add_fusion
  10.9 0.0 copy-start
  10.9 0.0 copy-start.1
  10.9 0.0 copy-start.2
  11.0 2.9 %collective-permute-start.1 = (f32[64,2048]{1,0:T(8,128)S(1)}, f32[64,2048]{1,0:T(8,128)}, u32[]{:S(2)}, u32[]{:S(2)}) collective-permute-start(f32[64,2048]{1,0:T(8,128)S(1)} %slice_bitcast_fusion), channel_id=1, source_target_pairs={{0,16},{8,24},{16,0},{24,8},{1,17},{9,25},{17,1},{25,9},{2,18},{10... | collective-permute-start | bytes 1572872 | tf_op jit(solution)/shard_map/ppermute | solution.py:37
  13.9 0.1 collective-permute-start.2
  14.0 12.3 %collective-permute-done.2 = f32[64]{0:T(128)S(1)} collective-permute-done((f32[64]{0:T(128)S(1)}, f32[64]{0:T(128)S(1)}, u32[]{:S(2)}, u32[]{:S(2)}) %collective-permute-start.2) | collective-permute-done | bytes 288 | tf_op jit(solution)/shard_map/ppermute | solution.py:41
  26.3 0.0 copy-done.3
  26.3 0.0 collective-permute-start.3
  26.9 0.5 %collective-permute-done.3 = f32[64]{0:T(128)S(1)} collective-permute-done((f32[64]{0:T(128)S(1)}, f32[64]{0:T(128)S(1)}, u32[]{:S(2)}, u32[]{:S(2)}) %collective-permute-start.3) | collective-permute-done | bytes 288 | tf_op jit(solution)/shard_map/ppermute | solution.py:42
  27.4 0.0 collective-permute-done.1
  27.5 1.9 %multiply_reduce_fusion = (f32[]{:T(128)}, f32[64,2048]{1,0:T(8,128)S(1)}) fusion(f32[64]{0:T(128)S(1)} %add_maximum_fusion, f32[64,2048]{1,0:T(8,128)} %collective-permute-done.1, f32[2,64,2048]{2,1,0:T(8,128)S(1)} %maximum_add_fusion), kind=kLoop, calls=%fused_computation.17 | loop fusion | flops 524287 | bytes 1573124 | tf_op jit(solution)/shard_map/reduce_sum | solution.py:46
  29.3 0.6 %compare_select_fusion.1 = f32[128]{0:T(128)S(1)} fusion(f32[]{:T(128)S(6)} %convert_element_type.24, f32[]{:T(128)} %get-tuple-element.7), kind=kLoop, calls=%fused_computation.21 | loop fusion | flops 512 | bytes 520 | tf_op jit(solution)/shard_map/jit(_where)/select_n | solution.py:48
  30.0 0.6 %broadcast_in_dim.38 = f32[32,1,128]{2,1,0:T(1,128)} broadcast(f32[128]{0:T(128)S(1)} %compare_select_fusion.1), dimensions={2} | broadcast | bytes 16896 | tf_op jit(solution)/shard_map/broadcast_in_dim | solution.py:50
  30.6 6.1 %all-to-all-start = ((f32[32,1,128]{2,1,0:T(1,128)}), f32[32,1,128]{2,1,0:T(1,128)S(1)}, u32[]{:S(2)}, u32[]{:S(2)}) async-start(f32[32,1,128]{2,1,0:T(1,128)} %broadcast_in_dim.38), calls=%async_computation | async-start | bytes 32768 | tf_op jit(solution)/shard_map/all_to_all | solution.py:50
  37.4 6.3 %all-to-all-done = f32[32,1,128]{2,1,0:T(1,128)S(1)} async-done(((f32[32,1,128]{2,1,0:T(1,128)}), f32[32,1,128]{2,1,0:T(1,128)S(1)}, u32[]{:S(2)}, u32[]{:S(2)}) %all-to-all-start) | async-done | bytes 16416 | tf_op jit(solution)/shard_map/all_to_all | solution.py:50
  43.8 0.6 %fusion.10 = (f32[1,1]{1,0:T(1,128)}, f32[1,1]{1,0:T(1,128)}) fusion(f32[1,128]{1,0:T(1,128)S(1)} %bitcast.60), kind=kLoop, calls=%fused_computation.25 | loop fusion | bytes 16 | tf_op jit(solution)/shard_map/slice | solution.py:52
  45.7 0.0 copy-done
  45.7 0.0 copy-done.1
  45.8 0.0 copy-done.2
  45.8 1.7 %fusion.4 = (f32[1,1,64,2048]{3,2,1,0:T(8,128)}, f32[64,2048]{1,0:T(8,128)}, f32[1,1,64,2048]{3,2,1,0:T(8,128)}, f32[1,1,64,2048]{3,2,1,0:T(8,128)}) fusion(f32[1,1,64,2048]{3,2,1,0:T(8,128)S(1)} %copy-done, f32[]{:T(128)S(6)} %sub.36, f32[1,1,64,2048]{3,2,1,0:T(8,128)S(1)} %copy-done.1, f32[]{:T(128)S(6)} %sub.35, f32[64,2048]{1,0:T(8,128)S(1)} %get-tuple-element.8, ...), kind=kLoop, calls=%fused_computation.16 | loop fusion | flops 2097152 | bytes 4194316 | tf_op jit(solution)/shard_map/broadcast_in_dim | solution.py:69
  (4 shorter events, 0.1 us)
Async XLA Ops:
  7.9 2.8 %collective-permute-start = (f32[2,64,2048]{2,1,0:T(8,128)S(1)}, f32[2,64,2048]{2,1,0:T(8,128)S(1)}, u32[]{:S(2)}, u32[]{:S(2)}) collective-permute-start(f32[2,64,2048]{2,1,0:T(8,128)S(1)} %pad_maximum_fusion), channel_id=1, source_target_pairs={{0,8},{8,0},{16,24},{24,16},{1,9},{9,1},{17,25},{25,17},{2,10},{10... | collective-permute-start | bytes 3145736 | tf_op jit(solution)/shard_map/ppermute | solution.py:34
  10.8 15.5 %copy-start.3 = (s32[1,1,1,64]{3,2,1,0:T(1,128)S(1)}, s32[1,1,1,64]{3,2,1,0:T(1,128)}, u32[]{:S(2)}) copy-start(s32[1,1,1,64]{3,2,1,0:T(1,128)} %param.8) | copy-start | bytes 772
  10.9 34.8 %copy-start = (f32[1,1,64,2048]{3,2,1,0:T(8,128)S(1)}, f32[1,1,64,2048]{3,2,1,0:T(8,128)}, u32[]{:S(2)}) copy-start(f32[1,1,64,2048]{3,2,1,0:T(8,128)} %param.11) | copy-start | bytes 1572868
  10.9 34.8 %copy-start.1 = (f32[1,1,64,2048]{3,2,1,0:T(8,128)S(1)}, f32[1,1,64,2048]{3,2,1,0:T(8,128)}, u32[]{:S(2)}) copy-start(f32[1,1,64,2048]{3,2,1,0:T(8,128)} %param.13) | copy-start | bytes 1572868
  10.9 34.8 %copy-start.2 = (f32[1,1,64,2048]{3,2,1,0:T(8,128)S(1)}, f32[1,1,64,2048]{3,2,1,0:T(8,128)}, u32[]{:S(2)}) copy-start(f32[1,1,64,2048]{3,2,1,0:T(8,128)} %param.12) | copy-start | bytes 1572868
  11.0 16.5 %collective-permute-start.1 = (f32[64,2048]{1,0:T(8,128)S(1)}, f32[64,2048]{1,0:T(8,128)}, u32[]{:S(2)}, u32[]{:S(2)}) collective-permute-start(f32[64,2048]{1,0:T(8,128)S(1)} %slice_bitcast_fusion), channel_id=1, source_target_pairs={{0,16},{8,24},{16,0},{24,8},{1,17},{9,25},{17,1},{25,9},{2,18},{10... | collective-permute-start | bytes 1572872 | tf_op jit(solution)/shard_map/ppermute | solution.py:37
  13.9 12.3 %collective-permute-start.2 = (f32[64]{0:T(128)S(1)}, f32[64]{0:T(128)S(1)}, u32[]{:S(2)}, u32[]{:S(2)}) collective-permute-start(f32[64]{0:T(128)S(1)} %get-tuple-element.18), channel_id=1, source_target_pairs={{0,16},{8,24},{16,0},{24,8},{1,17},{9,25},{17,1},{25,9},{2,18},{10... | collective-permute-start | bytes 776 | tf_op jit(solution)/shard_map/ppermute | solution.py:41
  26.3 1.2 %collective-permute-start.3 = (f32[64]{0:T(128)S(1)}, f32[64]{0:T(128)S(1)}, u32[]{:S(2)}, u32[]{:S(2)}) collective-permute-start(f32[64]{0:T(128)S(1)} %fusion.7), channel_id=1, source_target_pairs={{0,8},{8,0},{16,24},{24,16},{1,9},{9,1},{17,25},{25,17},{2,10},{10... | collective-permute-start | bytes 776 | tf_op jit(solution)/shard_map/ppermute | solution.py:42
  30.6 13.1 %all-to-all-start = ((f32[32,1,128]{2,1,0:T(1,128)}), f32[32,1,128]{2,1,0:T(1,128)S(1)}, u32[]{:S(2)}, u32[]{:S(2)}) async-start(f32[32,1,128]{2,1,0:T(1,128)} %broadcast_in_dim.38), calls=%async_computation | async-start | bytes 32768 | tf_op jit(solution)/shard_map/all_to_all | solution.py:50

commit v2 on v0

v2 whole, which is shorter than its diff:
```python
import jax
import jax.numpy as jnp
from jax import lax
from jax.experimental import pallas as pl
from jax.experimental.pallas import tpu as pltpu
from jax.sharding import PartitionSpec as P

ALL = ("dp", "tensor", "pipe")
VMEM = pltpu.MemorySpace.VMEM
SMEM = pltpu.MemorySpace.SMEM
CHUNK = 8


def in_vmem():
    return pl.BlockSpec(memory_space=VMEM)


def in_smem():
    return pl.BlockSpec(memory_space=SMEM)


def anywhere():
    return pl.BlockSpec(memory_space=pl.ANY)


def hold(x):
    return pltpu.with_memory_space_constraint(x, VMEM)


def column(row):
    n = row.shape[1]
    rows = lax.broadcasted_iota(jnp.int32, (n, n), 0)
    cols = lax.broadcasted_iota(jnp.int32, (n, n), 1)
    return jnp.sum(jnp.where(rows == cols, jnp.broadcast_to(row, (n, n)), 0.0), axis=1, keepdims=True)


def take_blocks(grad, flags, owner_order, owners, replicas):
    rows, width = grad.shape
    cols = width // replicas
    pieces = rows // CHUNK

    def kernel(order_ref, flags_ref, grad_ref, out_ref, sems):
        me = lax.axis_index("dp")
        wanted = owners(me // 2, me % 2)

        def copies(k):
            start = pl.multiple_of(order_ref[wanted[k]] * cols, cols)
            return [
                pltpu.make_async_copy(
                    grad_ref.at[pl.ds(r * CHUNK, CHUNK), pl.ds(start, cols)],
                    out_ref.at[k, pl.ds(r * CHUNK, CHUNK)],
                    sems.at[k, r],
                )
                for r in range(pieces)
            ]

        started = [copies(k) for k in range(len(wanted))]
        for block in started:
            for copy in block:
                copy.start()
        kept = column((1 - flags_ref[...]).astype(jnp.float32))
        for k, block in enumerate(started):
            for r, copy in enumerate(block):
                copy.wait()
                at = pl.ds(r * CHUNK, CHUNK)
                out_ref[k, at] = out_ref[k, at] * kept[r * CHUNK:(r + 1) * CHUNK]

    count = len(owners(0, 0))
    return pl.pallas_call(
        kernel,
        out_shape=pltpu.VMEM((count, rows, cols), jnp.float32),
        in_specs=[in_smem(), in_vmem(), anywhere()],
        out_specs=in_vmem(),
        scratch_shapes=[pltpu.SemaphoreType.DMA((count, pieces))],
    )(owner_order, flags, grad)


def prefetch(step_count, master, moment_m, moment_v):
    def kernel(step_ref, w_ref, m_ref, v_ref, pw_ref, pm_ref, pv_ref, bias_ref, sems):
        pairs = ((m_ref, pm_ref), (v_ref, pv_ref), (w_ref, pw_ref))
        copies = [pltpu.make_async_copy(a, b, sems.at[i]) for i, (a, b) in enumerate(pairs)]
        for copy in copies:
            copy.start()
        lane = lax.broadcasted_iota(jnp.int32, (1, 128), 1)
        base = jnp.where(lane == 0, 0.9, 0.999).astype(jnp.float32)
        power = jnp.ones((1, 128), jnp.float32)
        steps = jnp.full((1, 128), step_ref[0], jnp.int32)
        for bit in range(31):
            power = jnp.where((steps >> bit) & 1 == 1, power * base, power)
            base = base * base
        bias_ref[...] = 1.0 - power
        for copy in copies:
            copy.wait()

    shape = master.shape
    return pl.pallas_call(
        kernel,
        out_shape=(
            pltpu.VMEM(shape, jnp.float32),
            pltpu.VMEM(shape, jnp.float32),
            pltpu.VMEM(shape, jnp.float32),
            pltpu.VMEM((1, 128), jnp.float32),
        ),
        in_specs=[in_smem(), anywhere(), anywhere(), anywhere()],
        out_specs=(in_vmem(), in_vmem(), in_vmem(), in_vmem()),
        scratch_shapes=[pltpu.SemaphoreType.DMA((3,))],
        name="prefetch",
    )(step_count, master, moment_m, moment_v)


def mean_and_squares(near, own_mate, arrived, count, flags, devices):
    rows, cols = near.shape

    def kernel(near_ref, mate_ref, count_ref, flags_ref, *refs):
        others, (grad_ref, row_ref) = refs[:-2], refs[-2:]
        scale = column(1.0 / jnp.maximum(count_ref[...], 1.0))
        squares = jnp.zeros((CHUNK, cols), jnp.float32)
        for r in range(rows // CHUNK):
            at = pl.ds(r * CHUNK, CHUNK)
            total = near_ref[at] + mate_ref[at]
            for other in others:
                total = total + other[at]
            part = total * scale[r * CHUNK:(r + 1) * CHUNK]
            grad_ref[at] = part
            squares = squares + part * part
        square = jnp.sum(jnp.sum(squares, axis=0, keepdims=True), axis=1, keepdims=True)
        dropped = jnp.sum(flags_ref[...].astype(jnp.float32), axis=1, keepdims=True)
        lane = lax.broadcasted_iota(jnp.int32, (1, 128), 1)
        row = jnp.where(lane == 0, square, jnp.where(lane == 1, dropped, 0.0))
        row_ref[...] = jnp.broadcast_to(row[None], (devices, 1, 128))

    return pl.pallas_call(
        kernel,
        out_shape=(pltpu.VMEM((rows, cols), jnp.float32), pltpu.VMEM((devices, 1, 128), jnp.float32)),
        in_specs=[in_vmem()] * (4 + len(arrived)),
        out_specs=(in_vmem(), in_vmem()),
        name="mean_and_squares",
    )(hold(near), hold(own_mate), count, flags, *map(hold, arrived))


def update(rows_of, grad, bias, weights, old_m, old_v, entries):
    rows, cols = grad.shape
    pieces = rows // CHUNK

    def kernel(rows_ref, grad_ref, bias_ref, w_ref, m_ref, v_ref, *refs):
        outs, dropped_ref, stages, sems = refs[:4], refs[4], refs[5:9], refs[9]
        totals = jnp.sum(rows_ref[...], axis=0)
        rms = jnp.sqrt(totals[:, 0:1] / entries)
        clip = jnp.minimum(1.0, 0.05 / (rms + 1e-06))
        m_scale = 1.0 / bias_ref[:, 0:1]
        v_scale = 1.0 / bias_ref[:, 1:2]
        started = []
        for r in range(pieces):
            at = pl.ds(r * CHUNK, CHUNK)
            g = grad_ref[at] * clip
            w = w_ref[at]
            new_m = 0.9 * m_ref[at] + 0.1 * g
            new_v = 0.999 * v_ref[at] + 0.001 * g * g
            direction = (new_m * m_scale) / (jnp.sqrt(new_v * v_scale) + 1e-08) + 0.1 * w
            values = (w - 0.001 * direction, new_m, new_v, direction)
            for i in range(4):
                stages[i][at] = values[i]
                copy = pltpu.make_async_copy(stages[i].at[at], outs[i].at[at], sems.at[i, r])
                copy.start()
                started.append(copy)
        dropped_ref[0] = jnp.sum(totals[:, 1:2]).astype(jnp.int32)
        for copy in started:
            copy.wait()

    shape = jax.ShapeDtypeStruct((rows, cols), jnp.float32)
    return pl.pallas_call(
        kernel,
        out_shape=(shape, shape, shape, shape, jax.ShapeDtypeStruct((1,), jnp.int32)),
        in_specs=[in_vmem()] * 6,
        out_specs=(anywhere(), anywhere(), anywhere(), anywhere(), in_smem()),
        scratch_shapes=[pltpu.VMEM((rows, cols), jnp.float32)] * 4 + [pltpu.SemaphoreType.DMA((4, pieces))],
        name="update",
    )(hold(rows_of), *map(hold, (grad, bias, weights, old_m, old_v)))


def body(grad_parts, drop_flags, owner_order, step_count, master, moment_m, moment_v):
    replicas = lax.axis_size("dp")
    chips = replicas // 2
    devices = lax.axis_size(ALL)
    flags = drop_flags[0, 0]
    local_grad = grad_parts[0, 0, 0]
    rows_here, width = local_grad.shape

    mate_pairs = [(j, j ^ 1) for j in range(replicas)]

    def along(step):
        return [(j, (j // 2 + step) % chips * 2 + j % 2) for j in range(replicas)]

    def far(chip, core):
        return [(chip + step) % chips * 2 + core for step in range(1, chips)]

    def near(chip, core):
        return [chip * 2 + core]

    def mates(owners):
        return lambda chip, core: owners(chip, 1 - core)

    def take(owners):
        return take_blocks(local_grad, flags, owner_order, owners, replicas)

    kept = (1 - flags).astype(jnp.float32)
    far_mate = take(mates(far))
    far_got = lax.ppermute(far_mate, "dp", mate_pairs)
    far_own = take(far)
    count = kept
    for step in range(1, chips):
        count = count + lax.ppermute(kept, "dp", along(step))
    far_sum = far_own + far_got
    arrived = []
    for step in range(1, chips):
        arrived.append(lax.ppermute(far_sum[step - 1], "dp", along(step)))
    near_mate = take(mates(near))[0]
    near_got = lax.ppermute(near_mate, "dp", mate_pairs)
    near_own = take(near)[0]
    weights, old_m, old_v, bias = prefetch(
        step_count.reshape(1), master[0, 0], moment_m[0, 0], moment_v[0, 0]
    )
    count = count + lax.ppermute(count, "dp", mate_pairs)
    grad, row = mean_and_squares(near_own, near_got, arrived, count, flags, devices)
    rows = lax.all_to_all(row, ALL, 0, 0, tiled=True)
    entries = rows_here * width * lax.axis_size("tensor") * lax.axis_size("pipe")
    new_master, new_m, new_v, direction, dropped = update(
        rows, grad, bias, weights, old_m, old_v, entries
    )
    return (
        new_master[None, None],
        new_m[None, None],
        new_v[None, None],
        direction[None, None],
        dropped.reshape(()),
    )


def solution(mesh):
    return jax.shard_map(
        body,
        mesh=mesh,
        in_specs=(
            P("dp", "pipe", "tensor", None, None),
            P("dp", "pipe", "tensor", None),
            P(),
            P(),
            P("pipe", "tensor", None, "dp"),
            P("pipe", "tensor", None, "dp"),
            P("pipe", "tensor", None, "dp"),
        ),
        out_specs=(
            P("pipe", "tensor", None, "dp"),
            P("pipe", "tensor", None, "dp"),
            P("pipe", "tensor", None, "dp"),
            P("pipe", "tensor", None, "dp"),
            P(),
        ),
        check_vma=False,
    )
```

time: 92.3 us -> 42 us (0.46)
  blocking collectives: 67.3 us -> 0 us
  waiting for transfers between devices: 0.01 us -> 17.1 us
  Pallas kernels: 0 us -> 12.5 us
  other arithmetic: 10.7 us -> 0.58 us
  starting transfers between devices: 4.26 us -> 9.98 us
  local copies, waits for them, and re-layouts: 4.94 us -> 0.01 us
  between operations: 4.63 us -> 1.36 us
    psum x2 -> x0, blocking collectives: 67.3 us -> none  [the longest x1 41.6 us: body(): lax.psum((jnp.sum(grad * grad), jnp.sum(flags).astype(jnp.float32)), ('dp...]
    pallas_call x0 -> x7, Pallas kernels: none -> 12.5 us  [the longest x4 7.29 us: take_blocks(): pl.pallas_call(kernel, out_shape=pltpu.VMEM((count, rows, cols), jnp.floa...]
    ppermute x0 -> x5, waiting for transfers between devices: none -> 12.1 us  [the longest x1 12.1 us: body(): count = count + lax.ppermute(kept, 'dp', along(step))]
    all_to_all x1, waiting for transfers between devices: 0.01 us -> 5.03 us  [body(): rows = lax.all_to_all(row, ALL, 0, 0, tiled=True)]
    ppermute x0 -> x5, starting transfers between devices: none -> 3.8 us  [the longest x1 3.06 us: body(): arrived.append(lax.ppermute(far_sum[step - 1], 'dp', along(step)))]
    sub x1 -> x0, other arithmetic: 2.86 us -> none  [body(): new_master = weights - 0.001 * direction]
    squeeze x1 -> x0, local copies, waits for them, and re-layouts: 2.67 us -> none  [body(): local_grad = grad_parts[0, 0, 0]]
    mul x1 -> x0, other arithmetic: 2.57 us -> none  [body(): term = local_grad * kept[:, None]]
  transfers between devices with their start and end apart: 1 -> 6, of which waited for: 0 -> 2; matrix products, arithmetic and copies ran while one was open for 0% -> 1% of each run, Pallas kernels for 0% -> 17%
where the time goes in v2:
time: 42 us; the launch traced here: 41.5 us
  waiting for transfers between devices  17.1 us (41%)
  Pallas kernels  12.5 us (30%)
  starting transfers between devices  9.98 us (24%)
  between operations  1.36 us (3%)
  other arithmetic  0.58 us (1%)
    ppermute x1, waiting for transfers between devices, body(): count = count + lax.ppermute(kept, 'dp', along(step))  12.1 us
    pallas_call x4, Pallas kernels, take_blocks(): pl.pallas_call(kernel, out_shape=pltpu.VMEM((count, rows, cols), jnp.floa...  7.29 us
    all_to_all x1, starting transfers between devices, body(): rows = lax.all_to_all(row, ALL, 0, 0, tiled=True)  6.18 us
    all_to_all x1, waiting for transfers between devices, body(): rows = lax.all_to_all(row, ALL, 0, 0, tiled=True)  5.03 us
    ppermute x1, starting transfers between devices, body(): arrived.append(lax.ppermute(far_sum[step - 1], 'dp', along(step)))  3.06 us
    pallas_call x1, Pallas kernels, update(): pl.pallas_call(kernel, out_shape=(shape, shape, shape, shape, jax.ShapeDt...  2.24 us
    pallas_call x1, Pallas kernels, mean_and_squares(): pl.pallas_call(kernel, out_shape=(pltpu.VMEM((rows, cols), jnp.float32),...  1.54 us
    pallas_call x1, Pallas kernels, prefetch(): pl.pallas_call(kernel, out_shape=(pltpu.VMEM(shape, jnp.float32), pltpu.V...  1.39 us
  transfers between devices with their start and end apart: 6, of which 2 were waited for; matrix products, arithmetic and copies ran while one was open for 1% of the time, Pallas kernels for 17%

profile of v2, /device:TPU:0, one launch (start us, length us, event | category | flops | bytes accessed | tf_op | source)
XLA Modules:
  0.0 41.5 jit_solution(14599848380687100061)
XLA Ops:
  0.6 1.8 %shard_map.113 = f32[1,64,2048]{2,1,0:T(8,128)S(1)} custom-call(s32[4]{0:T(128)} %order_ref.7, s32[1,64]{1,0:T(1,128)} %bitcast.28, f32[64,8192]{1,0:T(8,128)} %bitcast.21), custom_call_target="tpu_custom_call" | custom-call | tf_op jit(solution)/shard_map/pallas_call | solution.py:69
  2.5 0.6 %collective-permute-start.3 = (f32[1,64,2048]{2,1,0:T(8,128)S(1)}, f32[1,64,2048]{2,1,0:T(8,128)S(1)}, u32[]{:S(2)}, u32[]{:S(2)}) collective-permute-start(f32[1,64,2048]{2,1,0:T(8,128)S(1)} %shard_map.113), channel_id=1, source_target_pairs={{0,8},{8,0},{16,24},{24,16},{1,9},{9,1},{17,25},{25,17},{2,10},{10... | collective-permute-start | bytes 1572872 | tf_op jit(solution)/shard_map/ppermute | solution.py:208
  3.0 1.8 %shard_map.111 = f32[1,64,2048]{2,1,0:T(8,128)S(1)} custom-call(s32[4]{0:T(128)} %order_ref.7, s32[1,64]{1,0:T(1,128)} %bitcast.29, f32[64,8192]{1,0:T(8,128)} %bitcast.22), custom_call_target="tpu_custom_call" | custom-call | tf_op jit(solution)/shard_map/pallas_call | solution.py:69
  4.8 0.0 copy-start
  4.9 0.1 collective-permute-start
  4.9 1.8 %shard_map.112 = f32[1,64,2048]{2,1,0:T(8,128)S(1)} custom-call(s32[4]{0:T(128)} %order_ref.7, s32[1,64]{1,0:T(1,128)} %bitcast.30, f32[64,8192]{1,0:T(8,128)} %bitcast.23), custom_call_target="tpu_custom_call" | custom-call | tf_op jit(solution)/shard_map/pallas_call | solution.py:69
  6.8 0.0 collective-permute-done.3
  6.8 0.1 add_bitcast_fusion
  6.9 3.1 %collective-permute-start.4 = (f32[64,2048]{1,0:T(8,128)S(1)}, f32[64,2048]{1,0:T(8,128)S(1)}, u32[]{:S(2)}, u32[]{:S(2)}) collective-permute-start(f32[64,2048]{1,0:T(8,128)S(1)} %add_bitcast_fusion), channel_id=1, source_target_pairs={{0,16},{8,24},{16,0},{24,8},{1,17},{9,25},{17,1},{25,9},{2,18},{10... | collective-permute-start | bytes 1572872 | tf_op jit(solution)/shard_map/ppermute | solution.py:216
  9.9 0.0 copy-done
  9.9 0.1 collective-permute-start.1
  10.0 12.1 %collective-permute-done.1 = f32[1,64]{1,0:T(1,128)S(1)} collective-permute-done((f32[1,64]{1,0:T(1,128)S(1)}, f32[1,64]{1,0:T(1,128)S(1)}, u32[]{:S(2)}, u32[]{:S(2)}) %collective-permute-start.1) | collective-permute-done | bytes 288 | tf_op jit(solution)/shard_map/ppermute | solution.py:212
  22.1 0.0 collective-permute-start.2
  22.1 1.8 %shard_map.110 = f32[1,64,2048]{2,1,0:T(8,128)S(1)} custom-call(s32[4]{0:T(128)} %order_ref.7, s32[1,64]{1,0:T(1,128)} %bitcast.31, f32[64,8192]{1,0:T(8,128)} %bitcast.24), custom_call_target="tpu_custom_call" | custom-call | tf_op jit(solution)/shard_map/pallas_call | solution.py:69
  23.9 0.0 collective-permute-done.2
  24.0 0.5 %add.10.count_ref = f32[1,64]{1,0:T(1,128)} add(f32[1,64]{1,0:T(1,128)S(1)} %fusion, f32[1,64]{1,0:T(1,128)S(1)} %collective-permute-done.2) | non-fusion elementwise | flops 64 | bytes 768 | tf_op jit(solution)/shard_map/add | solution.py:223
  24.5 0.0 collective-permute-done.mate_ref
  24.5 0.0 collective-permute-done.4.refs_0_
  24.5 1.5 %mean_and_squares.1 = (f32[64,2048]{1,0:T(8,128)S(1)}, f32[32,1,128]{2,1,0:T(1,128)}) custom-call(f32[64,2048]{1,0:T(8,128)S(1)} %bitcast.19, f32[64,2048]{1,0:T(8,128)S(1)} %collective-permute-done.mate_ref, f32[1,64]{1,0:T(1,128)} %add.10.count_ref, s32[1,64]{1,0:T(1,128)} %bitcast.32, f32[64,2048]{1,0:T(8,128)S(1)} %collective-permute-done.4.refs_0_), custom_call_target="tpu_custom_call" | custom-call | tf_op jit(solution)/shard_map/mean_and_squares/pallas_call | solution.py:132
  26.0 6.2 %all-to-all-start = ((f32[32,1,128]{2,1,0:T(1,128)}), f32[32,1,128]{2,1,0:T(1,128)S(1)}, u32[]{:S(2)}, u32[]{:S(2)}) async-start(f32[32,1,128]{2,1,0:T(1,128)} %get-tuple-element.16), calls=%async_computation | async-start | bytes 32768 | tf_op jit(solution)/shard_map/all_to_all | solution.py:225
  32.9 1.4 %prefetch.1 = (f32[64,2048]{1,0:T(8,128)S(1)}, f32[64,2048]{1,0:T(8,128)S(1)}, f32[64,2048]{1,0:T(8,128)S(1)}, f32[1,128]{1,0:T(1,128)S(1)}) custom-call(s32[1]{0:T(128)} %bitcast.18.step_ref, f32[64,2048]{1,0:T(8,128)} %bitcast.25, f32[64,2048]{1,0:T(8,128)} %bitcast.26, f32[64,2048]{1,0:T(8,128)} %bitcast.27), custom_call_target="tpu_custom_call" | custom-call | tf_op jit(solution)/shard_map/prefetch/pallas_call | solution.py:96
  34.3 5.0 %all-to-all-done.rows_ref = f32[32,1,128]{2,1,0:T(1,128)S(1)} async-done(((f32[32,1,128]{2,1,0:T(1,128)}), f32[32,1,128]{2,1,0:T(1,128)S(1)}, u32[]{:S(2)}, u32[]{:S(2)}) %all-to-all-start) | async-done | bytes 16416 | tf_op jit(solution)/shard_map/all_to_all | solution.py:225
  39.3 2.2 %update.1 = (f32[64,2048]{1,0:T(8,128)}, f32[64,2048]{1,0:T(8,128)}, f32[64,2048]{1,0:T(8,128)}, f32[64,2048]{1,0:T(8,128)}, s32[1]{0:T(128)}) custom-call(f32[32,1,128]{2,1,0:T(1,128)S(1)} %all-to-all-done.rows_ref, f32[64,2048]{1,0:T(8,128)S(1)} %get-tuple-element.17.grad_ref, f32[1,128]{1,0:T(1,128)S(1)} %get-tuple-element.18.bias_ref, ...), custom_call_target="tpu_custom_call" | custom-call | tf_op jit(solution)/shard_map/update/pallas_call | solution.py:171
  (2 shorter events, 0.0 us)
Async XLA Ops:
  2.5 4.3 %collective-permute-start.3 = (f32[1,64,2048]{2,1,0:T(8,128)S(1)}, f32[1,64,2048]{2,1,0:T(8,128)S(1)}, u32[]{:S(2)}, u32[]{:S(2)}) collective-permute-start(f32[1,64,2048]{2,1,0:T(8,128)S(1)} %shard_map.113), channel_id=1, source_target_pairs={{0,8},{8,0},{16,24},{24,16},{1,9},{9,1},{17,25},{25,17},{2,10},{10... | collective-permute-start | bytes 1572872 | tf_op jit(solution)/shard_map/ppermute | solution.py:208
  4.8 5.1 %copy-start = (s32[1,1,1,64]{3,2,1,0:T(1,128)S(1)}, s32[1,1,1,64]{3,2,1,0:T(1,128)}, u32[]{:S(2)}) copy-start(s32[1,1,1,64]{3,2,1,0:T(1,128)} %param.8) | copy-start | bytes 772
  4.9 19.6 %collective-permute-start = (f32[64,2048]{1,0:T(8,128)S(1)}, f32[64,2048]{1,0:T(8,128)S(1)}, u32[]{:S(2)}, u32[]{:S(2)}) collective-permute-start(f32[64,2048]{1,0:T(8,128)S(1)} %bitcast.20), channel_id=1, source_target_pairs={{0,8},{8,0},{16,24},{24,16},{1,9},{9,1},{17,25},{25,17},{2,10},{10... | collective-permute-start | bytes 1572872 | tf_op jit(solution)/shard_map/ppermute | solution.py:218
  6.9 17.6 %collective-permute-start.4 = (f32[64,2048]{1,0:T(8,128)S(1)}, f32[64,2048]{1,0:T(8,128)S(1)}, u32[]{:S(2)}, u32[]{:S(2)}) collective-permute-start(f32[64,2048]{1,0:T(8,128)S(1)} %add_bitcast_fusion), channel_id=1, source_target_pairs={{0,16},{8,24},{16,0},{24,8},{1,17},{9,25},{17,1},{25,9},{2,18},{10... | collective-permute-start | bytes 1572872 | tf_op jit(solution)/shard_map/ppermute | solution.py:216
  9.9 12.2 %collective-permute-start.1 = (f32[1,64]{1,0:T(1,128)S(1)}, f32[1,64]{1,0:T(1,128)S(1)}, u32[]{:S(2)}, u32[]{:S(2)}) collective-permute-start(f32[1,64]{1,0:T(1,128)S(1)} %subtract_convert_fusion), channel_id=1, source_target_pairs={{0,16},{8,24},{16,0},{24,8},{1,17},{9,25},{17,1},{25,9},{2,18},{10... | collective-permute-start | bytes 776 | tf_op jit(solution)/shard_map/ppermute | solution.py:212
  22.1 1.8 %collective-permute-start.2 = (f32[1,64]{1,0:T(1,128)S(1)}, f32[1,64]{1,0:T(1,128)S(1)}, u32[]{:S(2)}, u32[]{:S(2)}) collective-permute-start(f32[1,64]{1,0:T(1,128)S(1)} %fusion), channel_id=1, source_target_pairs={{0,8},{8,0},{16,24},{24,16},{1,9},{9,1},{17,25},{25,17},{2,10},{10... | collective-permute-start | bytes 776 | tf_op jit(solution)/shard_map/ppermute | solution.py:223
  26.0 13.3 %all-to-all-start = ((f32[32,1,128]{2,1,0:T(1,128)}), f32[32,1,128]{2,1,0:T(1,128)S(1)}, u32[]{:S(2)}, u32[]{:S(2)}) async-start(f32[32,1,128]{2,1,0:T(1,128)} %get-tuple-element.16), calls=%async_computation | async-start | bytes 32768 | tf_op jit(solution)/shard_map/all_to_all | solution.py:225

commit v3 on v2

--- a/solution.py
+++ b/solution.py
@@ -5,6 +5,7 @@
 from jax.experimental.pallas import tpu as pltpu
 from jax.sharding import PartitionSpec as P
 
+
 ALL = ("dp", "tensor", "pipe")
 VMEM = pltpu.MemorySpace.VMEM
 SMEM = pltpu.MemorySpace.SMEM
@@ -39,7 +40,8 @@
     cols = width // replicas
     pieces = rows // CHUNK
 
-    def kernel(order_ref, flags_ref, grad_ref, out_ref, sems):
+    def kernel(order_ref, flags_ref, grad_ref, out_ref, flags_here, sems, flags_sem):
+        flags_copy = pltpu.make_async_copy(flags_ref, flags_here, flags_sem)
         me = lax.axis_index("dp")
         wanted = owners(me // 2, me % 2)
 
@@ -58,7 +60,9 @@
         for block in started:
             for copy in block:
                 copy.start()
-        kept = column((1 - flags_ref[...]).astype(jnp.float32))
+        flags_copy.start()
+        flags_copy.wait()
+        kept = column((1 - flags_here[...]).astype(jnp.float32))
         for k, block in enumerate(started):
             for r, copy in enumerate(block):
                 copy.wait()
@@ -69,9 +73,13 @@
     return pl.pallas_call(
         kernel,
         out_shape=pltpu.VMEM((count, rows, cols), jnp.float32),
-        in_specs=[in_smem(), in_vmem(), anywhere()],
+        in_specs=[in_smem(), anywhere(), anywhere()],
         out_specs=in_vmem(),
-        scratch_shapes=[pltpu.SemaphoreType.DMA((count, pieces))],
+        scratch_shapes=[
+            pltpu.VMEM(flags.shape, flags.dtype),
+            pltpu.SemaphoreType.DMA((count, pieces)),
+            pltpu.SemaphoreType.DMA(()),
+        ],
     )(owner_order, flags, grad)
 
 
@@ -108,10 +116,10 @@
     )(step_count, master, moment_m, moment_v)
 
 
-def mean_and_squares(near, own_mate, arrived, count, flags, devices):
+def mean_and_squares(near, own_mate, arrived, count, kept, devices):
     rows, cols = near.shape
 
-    def kernel(near_ref, mate_ref, count_ref, flags_ref, *refs):
+    def kernel(near_ref, mate_ref, count_ref, kept_ref, *refs):
         others, (grad_ref, row_ref) = refs[:-2], refs[-2:]
         scale = column(1.0 / jnp.maximum(count_ref[...], 1.0))
         squares = jnp.zeros((CHUNK, cols), jnp.float32)
@@ -124,7 +132,7 @@
             grad_ref[at] = part
             squares = squares + part * part
         square = jnp.sum(jnp.sum(squares, axis=0, keepdims=True), axis=1, keepdims=True)
-        dropped = jnp.sum(flags_ref[...].astype(jnp.float32), axis=1, keepdims=True)
+        dropped = jnp.sum(1.0 - kept_ref[...], axis=1, keepdims=True)
         lane = lax.broadcasted_iota(jnp.int32, (1, 128), 1)
         row = jnp.where(lane == 0, square, jnp.where(lane == 1, dropped, 0.0))
         row_ref[...] = jnp.broadcast_to(row[None], (devices, 1, 128))
@@ -135,7 +143,7 @@
         in_specs=[in_vmem()] * (4 + len(arrived)),
         out_specs=(in_vmem(), in_vmem()),
         name="mean_and_squares",
-    )(hold(near), hold(own_mate), count, flags, *map(hold, arrived))
+    )(*map(hold, (near, own_mate, count, kept, *arrived)))
 
 
 def update(rows_of, grad, bias, weights, old_m, old_v, entries):
@@ -143,8 +151,11 @@
     pieces = rows // CHUNK
 
     def kernel(rows_ref, grad_ref, bias_ref, w_ref, m_ref, v_ref, *refs):
-        outs, dropped_ref, stages, sems = refs[:4], refs[4], refs[5:9], refs[9]
+        outs, dropped_ref, stages, sems, dropped_here, dropped_sem = refs[:4], refs[4], refs[5:9], *refs[9:]
         totals = jnp.sum(rows_ref[...], axis=0)
+        dropped_here[...] = jnp.sum(totals[:, 1:2], axis=1, keepdims=True).astype(jnp.int32) + jnp.zeros((1, 128), jnp.int32)
+        dropped_copy = pltpu.make_async_copy(dropped_here, dropped_ref, dropped_sem)
+        dropped_copy.start()
         rms = jnp.sqrt(totals[:, 0:1] / entries)
         clip = jnp.minimum(1.0, 0.05 / (rms + 1e-06))
         m_scale = 1.0 / bias_ref[:, 0:1]
@@ -163,17 +174,17 @@
                 copy = pltpu.make_async_copy(stages[i].at[at], outs[i].at[at], sems.at[i, r])
                 copy.start()
                 started.append(copy)
-        dropped_ref[0] = jnp.sum(totals[:, 1:2]).astype(jnp.int32)
+        dropped_copy.wait()
         for copy in started:
             copy.wait()
 
     shape = jax.ShapeDtypeStruct((rows, cols), jnp.float32)
     return pl.pallas_call(
         kernel,
-        out_shape=(shape, shape, shape, shape, jax.ShapeDtypeStruct((1,), jnp.int32)),
+        out_shape=(shape, shape, shape, shape, jax.ShapeDtypeStruct((1, 128), jnp.int32)),
         in_specs=[in_vmem()] * 6,
-        out_specs=(anywhere(), anywhere(), anywhere(), anywhere(), in_smem()),
-        scratch_shapes=[pltpu.VMEM((rows, cols), jnp.float32)] * 4 + [pltpu.SemaphoreType.DMA((4, pieces))],
+        out_specs=(anywhere(), anywhere(), anywhere(), anywhere(), anywhere()),
+        scratch_shapes=[pltpu.VMEM((rows, cols), jnp.float32)] * 4 + [pltpu.SemaphoreType.DMA((4, pieces)), pltpu.VMEM((1, 128), jnp.int32), pltpu.SemaphoreType.DMA(())],
         name="update",
     )(hold(rows_of), *map(hold, (grad, bias, weights, old_m, old_v)))
 
@@ -221,7 +232,7 @@
         step_count.reshape(1), master[0, 0], moment_m[0, 0], moment_v[0, 0]
     )
     count = count + lax.ppermute(count, "dp", mate_pairs)
-    grad, row = mean_and_squares(near_own, near_got, arrived, count, flags, devices)
+    grad, row = mean_and_squares(near_own, near_got, arrived, count, kept, devices)
     rows = lax.all_to_all(row, ALL, 0, 0, tiled=True)
     entries = rows_here * width * lax.axis_size("tensor") * lax.axis_size("pipe")
     new_master, new_m, new_v, direction, dropped = update(
@@ -232,7 +243,7 @@
         new_m[None, None],
         new_v[None, None],
         direction[None, None],
-        dropped.reshape(()),
+        dropped[0, 0],
     )
 
 

time: 42 us -> 40.4 us (0.962)
  Pallas kernels: 12.5 us -> 11.3 us
  other arithmetic: 0.58 us -> 0.08 us
    pallas_call x1, Pallas kernels: 1.54 us -> 0.88 us  [mean_and_squares(): pl.pallas_call(kernel, out_shape=(pltpu.VMEM((rows, cols), jnp.float32),...]
    add x1, other arithmetic: 0.51 us -> 0.01 us  [body(): count = count + lax.ppermute(count, 'dp', mate_pairs)]
    pallas_call x1, Pallas kernels: 2.24 us -> 1.73 us  [update(): pl.pallas_call(kernel, out_shape=(shape, shape, shape, shape, jax.ShapeDt...]
  transfers between devices with their start and end apart: 6 -> 6, of which waited for: 2 -> 2; matrix products, arithmetic and copies ran while one was open for 1% -> 0% of each run, Pallas kernels for 17% -> 17%
where the time goes in v3:
time: 40.4 us; the launch traced here: 39.9 us
  waiting for transfers between devices  17.1 us (42%)
  Pallas kernels  11.3 us (28%)
  starting transfers between devices  9.98 us (25%)
  between operations  1.38 us (3%)
    ppermute x1, waiting for transfers between devices, body(): count = count + lax.ppermute(kept, 'dp', along(step))  12.1 us
    pallas_call x4, Pallas kernels, take_blocks(): pl.pallas_call(kernel, out_shape=pltpu.VMEM((count, rows, cols), jnp.floa...  7.34 us
    all_to_all x1, starting transfers between devices, body(): rows = lax.all_to_all(row, ALL, 0, 0, tiled=True)  6.18 us
    all_to_all x1, waiting for transfers between devices, body(): rows = lax.all_to_all(row, ALL, 0, 0, tiled=True)  5.03 us
    ppermute x1, starting transfers between devices, body(): arrived.append(lax.ppermute(far_sum[step - 1], 'dp', along(step)))  3.06 us
    pallas_call x1, Pallas kernels, update(): pl.pallas_call(kernel, out_shape=(shape, shape, shape, shape, jax.ShapeDt...  1.73 us
    pallas_call x1, Pallas kernels, prefetch(): pl.pallas_call(kernel, out_shape=(pltpu.VMEM(shape, jnp.float32), pltpu.V...  1.39 us
    pallas_call x1, Pallas kernels, mean_and_squares(): pl.pallas_call(kernel, out_shape=(pltpu.VMEM((rows, cols), jnp.float32),...  0.88 us
  transfers between devices with their start and end apart: 6, of which 2 were waited for; matrix products, arithmetic and copies ran while one was open for 0% of the time, Pallas kernels for 17%

profile of v3, /device:TPU:0, one launch (start us, length us, event | category | flops | bytes accessed | tf_op | source)
XLA Modules:
  0.0 39.9 jit_solution(14998846467102769244)
XLA Ops:
  0.6 1.8 %shard_map.113 = f32[1,64,2048]{2,1,0:T(8,128)S(1)} custom-call(s32[4]{0:T(128)} %order_ref.7, s32[1,64]{1,0:T(1,128)} %bitcast.29, f32[64,8192]{1,0:T(8,128)} %bitcast.22), custom_call_target="tpu_custom_call" | custom-call | tf_op jit(solution)/shard_map/pallas_call | solution.py:73
  2.5 0.6 %collective-permute-start.3 = (f32[1,64,2048]{2,1,0:T(8,128)S(1)}, f32[1,64,2048]{2,1,0:T(8,128)S(1)}, u32[]{:S(2)}, u32[]{:S(2)}) collective-permute-start(f32[1,64,2048]{2,1,0:T(8,128)S(1)} %shard_map.113), channel_id=1, source_target_pairs={{0,8},{8,0},{16,24},{24,16},{1,9},{9,1},{17,25},{25,17},{2,10},{10... | collective-permute-start | bytes 1572872 | tf_op jit(solution)/shard_map/ppermute | solution.py:219
  3.0 1.8 %shard_map.111 = f32[1,64,2048]{2,1,0:T(8,128)S(1)} custom-call(s32[4]{0:T(128)} %order_ref.7, s32[1,64]{1,0:T(1,128)} %bitcast.30, f32[64,8192]{1,0:T(8,128)} %bitcast.23), custom_call_target="tpu_custom_call" | custom-call | tf_op jit(solution)/shard_map/pallas_call | solution.py:73
  4.9 0.0 copy-start
  4.9 0.1 collective-permute-start
  5.0 1.8 %shard_map.112 = f32[1,64,2048]{2,1,0:T(8,128)S(1)} custom-call(s32[4]{0:T(128)} %order_ref.7, s32[1,64]{1,0:T(1,128)} %bitcast.31, f32[64,8192]{1,0:T(8,128)} %bitcast.24), custom_call_target="tpu_custom_call" | custom-call | tf_op jit(solution)/shard_map/pallas_call | solution.py:73
  6.8 0.0 collective-permute-done.3
  6.8 0.1 add_bitcast_fusion
  6.9 3.1 %collective-permute-start.4 = (f32[64,2048]{1,0:T(8,128)S(1)}, f32[64,2048]{1,0:T(8,128)S(1)}, u32[]{:S(2)}, u32[]{:S(2)}) collective-permute-start(f32[64,2048]{1,0:T(8,128)S(1)} %add_bitcast_fusion), channel_id=1, source_target_pairs={{0,16},{8,24},{16,0},{24,8},{1,17},{9,25},{17,1},{25,9},{2,18},{10... | collective-permute-start | bytes 1572872 | tf_op jit(solution)/shard_map/ppermute | solution.py:227
  10.0 0.0 copy-done
  10.0 0.1 collective-permute-start.1
  10.1 12.1 %collective-permute-done.1 = f32[1,64]{1,0:T(1,128)S(1)} collective-permute-done((f32[1,64]{1,0:T(1,128)S(1)}, f32[1,64]{1,0:T(1,128)S(1)}, u32[]{:S(2)}, u32[]{:S(2)}) %collective-permute-start.1) | collective-permute-done | bytes 288 | tf_op jit(solution)/shard_map/ppermute | solution.py:223
  22.2 0.0 collective-permute-start.2
  22.2 1.8 %shard_map.110 = f32[1,64,2048]{2,1,0:T(8,128)S(1)} custom-call(s32[4]{0:T(128)} %order_ref.7, s32[1,64]{1,0:T(1,128)} %bitcast.32, f32[64,8192]{1,0:T(8,128)} %bitcast.25), custom_call_target="tpu_custom_call" | custom-call | tf_op jit(solution)/shard_map/pallas_call | solution.py:73
  24.0 0.0 collective-permute-done.2
  24.0 0.0 collective-permute-done.mate_ref
  24.0 0.0 collective-permute-done.4.refs_0_
  24.1 0.9 %mean_and_squares.1 = (f32[64,2048]{1,0:T(8,128)S(1)}, f32[32,1,128]{2,1,0:T(1,128)}) custom-call(f32[64,2048]{1,0:T(8,128)S(1)} %bitcast.20, f32[64,2048]{1,0:T(8,128)S(1)} %collective-permute-done.mate_ref, f32[1,64]{1,0:T(1,128)S(1)} %add.10.count_ref, f32[1,64]{1,0:T(1,128)S(1)} %subtract_convert_fusion.kept_ref, ...), custom_call_target="tpu_custom_call" | custom-call | tf_op jit(solution)/shard_map/mean_and_squares/pallas_call | solution.py:140
  24.9 6.2 %all-to-all-start = ((f32[32,1,128]{2,1,0:T(1,128)}), f32[32,1,128]{2,1,0:T(1,128)S(1)}, u32[]{:S(2)}, u32[]{:S(2)}) async-start(f32[32,1,128]{2,1,0:T(1,128)} %get-tuple-element.16), calls=%async_computation | async-start | bytes 32768 | tf_op jit(solution)/shard_map/all_to_all | solution.py:236
  31.8 1.4 %prefetch.1 = (f32[64,2048]{1,0:T(8,128)S(1)}, f32[64,2048]{1,0:T(8,128)S(1)}, f32[64,2048]{1,0:T(8,128)S(1)}, f32[1,128]{1,0:T(1,128)S(1)}) custom-call(s32[1]{0:T(128)} %bitcast.19.step_ref, f32[64,2048]{1,0:T(8,128)} %bitcast.26, f32[64,2048]{1,0:T(8,128)} %bitcast.27, f32[64,2048]{1,0:T(8,128)} %bitcast.28), custom_call_target="tpu_custom_call" | custom-call | tf_op jit(solution)/shard_map/prefetch/pallas_call | solution.py:104
  33.2 5.0 %all-to-all-done.rows_ref = f32[32,1,128]{2,1,0:T(1,128)S(1)} async-done(((f32[32,1,128]{2,1,0:T(1,128)}), f32[32,1,128]{2,1,0:T(1,128)S(1)}, u32[]{:S(2)}, u32[]{:S(2)}) %all-to-all-start) | async-done | bytes 16416 | tf_op jit(solution)/shard_map/all_to_all | solution.py:236
  38.2 1.7 %update.1 = (f32[64,2048]{1,0:T(8,128)}, f32[64,2048]{1,0:T(8,128)}, f32[64,2048]{1,0:T(8,128)}, f32[64,2048]{1,0:T(8,128)}, s32[1,128]{1,0:T(1,128)}) custom-call(f32[32,1,128]{2,1,0:T(1,128)S(1)} %all-to-all-done.rows_ref, f32[64,2048]{1,0:T(8,128)S(1)} %get-tuple-element.17.grad_ref, f32[1,128]{1,0:T(1,128)S(1)} %get-tuple-element.18.bias_ref, ...), custom_call_target="tpu_custom_call" | custom-call | tf_op jit(solution)/shard_map/update/pallas_call | solution.py:182
  (3 shorter events, 0.0 us)
Async XLA Ops:
  2.5 4.3 %collective-permute-start.3 = (f32[1,64,2048]{2,1,0:T(8,128)S(1)}, f32[1,64,2048]{2,1,0:T(8,128)S(1)}, u32[]{:S(2)}, u32[]{:S(2)}) collective-permute-start(f32[1,64,2048]{2,1,0:T(8,128)S(1)} %shard_map.113), channel_id=1, source_target_pairs={{0,8},{8,0},{16,24},{24,16},{1,9},{9,1},{17,25},{25,17},{2,10},{10... | collective-permute-start | bytes 1572872 | tf_op jit(solution)/shard_map/ppermute | solution.py:219
  4.9 5.1 %copy-start = (s32[1,1,1,64]{3,2,1,0:T(1,128)S(1)}, s32[1,1,1,64]{3,2,1,0:T(1,128)}, u32[]{:S(2)}) copy-start(s32[1,1,1,64]{3,2,1,0:T(1,128)} %param.8) | copy-start | bytes 772
  4.9 19.1 %collective-permute-start = (f32[64,2048]{1,0:T(8,128)S(1)}, f32[64,2048]{1,0:T(8,128)S(1)}, u32[]{:S(2)}, u32[]{:S(2)}) collective-permute-start(f32[64,2048]{1,0:T(8,128)S(1)} %bitcast.21), channel_id=1, source_target_pairs={{0,8},{8,0},{16,24},{24,16},{1,9},{9,1},{17,25},{25,17},{2,10},{10... | collective-permute-start | bytes 1572872 | tf_op jit(solution)/shard_map/ppermute | solution.py:229
  6.9 17.1 %collective-permute-start.4 = (f32[64,2048]{1,0:T(8,128)S(1)}, f32[64,2048]{1,0:T(8,128)S(1)}, u32[]{:S(2)}, u32[]{:S(2)}) collective-permute-start(f32[64,2048]{1,0:T(8,128)S(1)} %add_bitcast_fusion), channel_id=1, source_target_pairs={{0,16},{8,24},{16,0},{24,8},{1,17},{9,25},{17,1},{25,9},{2,18},{10... | collective-permute-start | bytes 1572872 | tf_op jit(solution)/shard_map/ppermute | solution.py:227
  10.0 12.2 %collective-permute-start.1 = (f32[1,64]{1,0:T(1,128)S(1)}, f32[1,64]{1,0:T(1,128)S(1)}, u32[]{:S(2)}, u32[]{:S(2)}) collective-permute-start(f32[1,64]{1,0:T(1,128)S(1)} %subtract_convert_fusion.kept_ref), channel_id=1, source_target_pairs={{0,16},{8,24},{16,0},{24,8},{1,17},{9,25},{17,1},{25,9},{2,18},{10... | collective-permute-start | bytes 776 | tf_op jit(solution)/shard_map/ppermute | solution.py:223
  22.2 1.8 %collective-permute-start.2 = (f32[1,64]{1,0:T(1,128)S(1)}, f32[1,64]{1,0:T(1,128)S(1)}, u32[]{:S(2)}, u32[]{:S(2)}) collective-permute-start(f32[1,64]{1,0:T(1,128)S(1)} %fusion), channel_id=1, source_target_pairs={{0,8},{8,0},{16,24},{24,16},{1,9},{9,1},{17,25},{25,17},{2,10},{10... | collective-permute-start | bytes 776 | tf_op jit(solution)/shard_map/ppermute | solution.py:234
  24.9 13.3 %all-to-all-start = ((f32[32,1,128]{2,1,0:T(1,128)}), f32[32,1,128]{2,1,0:T(1,128)S(1)}, u32[]{:S(2)}, u32[]{:S(2)}) async-start(f32[32,1,128]{2,1,0:T(1,128)} %get-tuple-element.16), calls=%async_computation | async-start | bytes 32768 | tf_op jit(solution)/shard_map/all_to_all | solution.py:236
